TPU v7x, 32 devices: a whole 2x2x4 slice. The times are simulated.
32 devices in a mesh: row: 8 (over z, core), col: 4 (over y, x).
Axes of the slice: x: 2, y: 2, z: 4, core: 2. Of those that a mesh axis runs over, the one named last changes fastest.
Arguments:
- pair_exchange: bfloat16 [64, 16, 1024], P(('row', 'col')), may hold values from -6 to 6
- conduction: bfloat16 [64, 4, 1024], P(('row', 'col')), may hold values from -6 to 6
- valence: bfloat16 [64, 4, 1024], P(('row', 'col')), may hold values from -6 to 6
- coulomb: float32 [1024], replicated, may hold values from 0.5 to 5
- screening: float32 [34, 1024], replicated, may hold values from 0.1 to 1
- energies: float32 [64, 16], P(('row', 'col')), may hold values from 1 to 9
- vectors: bfloat16 [64, 512], P(('row', 'col')), may hold values from -6 to 6
- k_coords: int32 [64, 2], P(('row', 'col')), may hold values from 0 to 31, as said below
Outputs:
- residual_block: float32 [64, 512], P(('row', 'col'))
- alpha: float32 [32, 32], replicated
Inputs may be any that keep to these rules, and one draw needn't show every extreme that they name: `k_coords`: each row holds a k-point's coordinates on the periodic 32 x 2 mesh, first then second; every mesh point occurs exactly once.
All inputs are finite; a program needn't handle non-finite values.
Results may differ from a plain program's by a relative error of at most 0.0028.
Values may be sent and summed in bfloat16 or wider, within the bound.
A program may use at most 64 MiB of HBM per device.

v0:
```python
import jax
import jax.numpy as jnp
from jax import lax
from jax.sharding import PartitionSpec as P

MX = 32
highest = lax.Precision.HIGHEST


def pair_factors(conduction, valence):
    count, valence_count, plane_count = valence.shape
    joined = (
        valence.astype(jnp.float32)[:, :, None, :] * conduction.astype(jnp.float32)[:, None, :, :]
    )
    return joined.reshape(count, valence_count * conduction.shape[1], plane_count).astype(
        jnp.bfloat16
    )


def transfer_index(rows_at, cols_at, mesh_cols):
    delta_first = jnp.mod(rows_at[:, None, 0] - cols_at[None, :, 0], MX)
    delta_second = jnp.mod(rows_at[:, None, 1] - cols_at[None, :, 1], mesh_cols)
    fold_first = jnp.minimum(delta_first, MX - delta_first)
    fold_second = jnp.minimum(delta_second, mesh_cols - delta_second)
    return (fold_first * (mesh_cols // 2 + 1) + fold_second).astype(jnp.int32)


def on_device(pair_exchange, conduction, valence, coulomb, screening, energies, vectors, k_coords):
    local_count, band_count, plane_count = pair_exchange.shape
    vector_count = vectors.shape[1] // band_count
    row_count = lax.axis_size("row")
    col_count = lax.axis_size("col")
    total_count = local_count * row_count * col_count
    mesh_cols = total_count // MX
    moving = vectors.reshape(local_count, band_count, vector_count)
    partial_density = jnp.einsum(
        "ktg,ktn->gn", pair_exchange, moving, preferred_element_type=jnp.float32
    )
    density = lax.psum(partial_density, ("row", "col"))
    block_size = 128
    sweeps = plane_count // block_size
    col_cond, col_val, col_vec, col_at = (
        lax.all_gather(conduction, "row", axis=0, tiled=True),
        lax.all_gather(valence, "row", axis=0, tiled=True),
        lax.all_gather(vectors, "row", axis=0, tiled=True),
        lax.all_gather(k_coords, "row", axis=0, tiled=True),
    )
    row_cond, row_val, row_at = (
        lax.all_gather(conduction, "col", axis=0, tiled=True),
        lax.all_gather(valence, "col", axis=0, tiled=True),
        lax.all_gather(k_coords, "col", axis=0, tiled=True),
    )
    row_pairs = pair_factors(row_cond, row_val)
    col_pairs = pair_factors(col_cond, col_val)
    indices = transfer_index(row_at, col_at, mesh_cols)
    col_moving = col_vec.reshape(-1, band_count, vector_count)

    def square_sweep(sweep_index, running):
        anchor = sweep_index * block_size
        coupling = jnp.take(
            lax.dynamic_slice_in_dim(screening, anchor, block_size, 1), indices, axis=0
        )
        row_block = lax.dynamic_slice_in_dim(row_pairs, anchor, block_size, 2)
        col_block = lax.dynamic_slice_in_dim(col_pairs, anchor, block_size, 2)
        col_proj = jnp.einsum(
            "ktg,ktn->kng", col_block, col_moving, preferred_element_type=jnp.float32
        )
        potential = jnp.einsum("ijg,jng->ing", coupling, col_proj, precision=highest)
        return running + jnp.einsum(
            "ktg,kng->ktn", row_block.astype(jnp.float32), potential, precision=highest
        )

    forward = lax.fori_loop(
        0,
        sweeps,
        square_sweep,
        jnp.zeros((row_pairs.shape[0], band_count, vector_count), jnp.float32),
    )
    owned = lax.psum_scatter(
        forward.reshape(col_count, local_count, band_count, vector_count),
        "col",
        scatter_dimension=0,
        tiled=True,
    )[0]
    moving_wide = moving.astype(jnp.float32)
    exchange_term = jnp.einsum(
        "ktg,gn->ktn", pair_exchange.astype(jnp.float32) * coulomb, density, precision=highest
    )
    applied = (
        energies[:, :, None] * moving_wide
        + 2.0 / (total_count * band_count) * exchange_term
        - owned / total_count
    )
    gram = jnp.einsum("ktm,ktn->mn", moving_wide, applied, precision=highest)
    alpha = lax.psum(gram, ("row", "col")) / (total_count * band_count)
    residual = applied - jnp.einsum("ktm,mn->ktn", moving_wide, alpha, precision=highest)
    return (residual.reshape(local_count, band_count * vector_count), alpha)


def solution(mesh):
    in_specs = (
        P(("row", "col"), None, None),
        P(("row", "col"), None, None),
        P(("row", "col"), None, None),
        P(),
        P(),
        P(("row", "col"), None),
        P(("row", "col"), None),
        P(("row", "col"), None),
    )
    out_specs = (P(("row", "col"), None), P())
    return jax.shard_map(
        on_device, mesh=mesh, in_specs=in_specs, out_specs=out_specs, check_vma=False
    )
```

profile of v0, /device:TPU:0, one launch (start us, length us, event | category | flops | bytes accessed | tf_op | source)
XLA Modules:
  0.0 299.9 jit_solution(13418184121838847277)
XLA Ops:
  8.7 13.5 %all-gather.2 = s32[8,2,2]{2,1,0:T(2,128)S(1)} all-gather(s32[1,2,2]{2,1,0:T(2,128)S(1)} %bitcast.65), channel_id=1, replica_groups=mesh['row'=8,'col'=4] {'row'}, dimensions={0}, use_global_device_ids=true | all-gather | bytes 144 | tf_op jit(solution)/shard_map/all_gather | solution.py:46
  22.1 8.1 %all-gather.1 = s32[4,2,2]{2,1,0:T(2,128)S(1)} all-gather(s32[1,2,2]{2,1,0:T(2,128)S(1)} %bitcast.66), channel_id=1, replica_groups=mesh['row'=8,'col'=4] {'col'}, dimensions={0}, use_global_device_ids=true | all-gather | bytes 80 | tf_op jit(solution)/shard_map/all_gather | solution.py:51
  30.2 14.3 %all_gather.23 = bf16[16,4,1024]{2,1,0:T(4,128)(2,1)S(1)} all-gather(bf16[2,4,1024]{2,1,0:T(4,128)(2,1)} %param.12), channel_id=1, replica_groups=mesh['row'=8,'col'=4] {'row'}, dimensions={0}, use_global_device_ids=true | all-gather | bytes 147456 | tf_op jit(solution)/shard_map/all_gather | solution.py:44
  44.5 8.3 %all_gather.21 = bf16[8,4,1024]{2,1,0:T(4,128)(2,1)S(1)} all-gather(bf16[2,4,1024]{2,1,0:T(4,128)(2,1)S(1)} %copy-done.2), channel_id=1, replica_groups=mesh['row'=8,'col'=4] {'col'}, dimensions={0}, use_global_device_ids=true | all-gather | bytes 81920 | tf_op jit(solution)/shard_map/all_gather | solution.py:50
  52.9 14.0 %all_gather.24 = bf16[16,4,1024]{2,1,0:T(4,128)(2,1)S(1)} all-gather(bf16[2,4,1024]{2,1,0:T(4,128)(2,1)S(1)} %copy-done.3), channel_id=1, replica_groups=mesh['row'=8,'col'=4] {'row'}, dimensions={0}, use_global_device_ids=true | all-gather | bytes 147456 | tf_op jit(solution)/shard_map/all_gather | solution.py:43
  66.9 7.2 %all_gather.22 = bf16[8,4,1024]{2,1,0:T(4,128)(2,1)S(1)} all-gather(bf16[2,4,1024]{2,1,0:T(4,128)(2,1)S(1)} %copy-done.3), channel_id=1, replica_groups=mesh['row'=8,'col'=4] {'col'}, dimensions={0}, use_global_device_ids=true | all-gather | bytes 81920 | tf_op jit(solution)/shard_map/all_gather | solution.py:49
  75.8 12.8 %all-gather = bf16[8,2,512]{2,1,0:T(2,128)(2,1)S(1)} all-gather(bf16[1,2,512]{2,1,0:T(2,128)(2,1)S(1)} %bitcast.64), channel_id=1, replica_groups=mesh['row'=8,'col'=4] {'row'}, dimensions={0}, use_global_device_ids=true | all-gather | bytes 18432 | tf_op jit(solution)/shard_map/all_gather | solution.py:45
  88.7 33.2 %while.14 = (s32[]{:T(128)}, f32[8,16,32]{2,1,0:T(8,128)S(1)}, bf16[8,16,1024]{2,1,0:T(8,128)(2,1)S(1)}, bf16[16,16,1024]{2,1,0:T(8,128)(2,1)S(1)}, bf16[16,16,3...) while((s32[]{:T(128)}, f32[8,16,32]{2,1,0:T(8,128)S(1)}, ...), condition=%wide.region_2.3_spmd.clone, body=%wide.region_1.2_spmd.clone.sunk | while | flops 14714503 | bytes 2319689 | solution.py:73
  88.7 0.7 constant_dynamic-slice_fusion.2
  89.6 0.6 gather_fusion
  91.4 1.1 convolution_bitcast_fusion.8
  92.9 0.7 constant_dynamic-slice_fusion.2
  95.5 1.1 convolution_bitcast_fusion.8
  97.0 0.7 constant_dynamic-slice_fusion.2
  99.7 1.1 convolution_bitcast_fusion.8
  101.2 0.7 constant_dynamic-slice_fusion.2
  103.8 1.1 convolution_bitcast_fusion.8
  105.3 0.7 constant_dynamic-slice_fusion.2
  108.0 1.1 convolution_bitcast_fusion.8
  109.5 0.7 constant_dynamic-slice_fusion.2
  112.1 1.1 convolution_bitcast_fusion.8
  113.6 0.7 constant_dynamic-slice_fusion.2
  116.3 1.1 convolution_bitcast_fusion.8
  117.8 0.7 constant_dynamic-slice_fusion.2
  120.4 1.1 convolution_bitcast_fusion.8
  122.8 0.9 convolution_bitcast_fusion.2
  123.7 20.8 %reduce-scatter.4.cloned.1.call-done = f32[1,2,16,32]{3,2,1,0:T(8,128)} async-done(((f32[4,2,16,32]{3,2,1,0:T(8,128)}), f32[1,2,16,32]{3,2,1,0:T(8,128)}) %reduce-scatter.4.cloned.1.call-update) | async-done | bytes 4112
  144.5 105.8 %all-reduce.3.cloned.1.call-done = f32[1024,32]{0,1:T(8,128)} async-done(((f32[1024,32]{0,1:T(8,128)}), f32[1024,32]{0,1:T(8,128)}) %all-reduce.3.cloned.1.call-update) | async-done | bytes 131088 | tf_op jit(solution)/shard_map/psum | solution.py:39
  250.3 1.1 fusion.17
  251.7 39.3 %psum.15 = f32[32,32]{0,1:T(8,128)S(1)} all-reduce(f32[32,32]{0,1:T(8,128)S(1)} %convolution_bitcast_fusion.4), channel_id=1, replica_groups=mesh['row'=8,'col'=4] {'row','col'}, use_global_device_ids=true, to_apply=%region_4.5 | all-reduce | flops 1024 | bytes 8192 | tf_op jit(solution)/shard_map/psum | solution.py:95
  291.1 0.7 reshape.61
  291.8 0.7 copy.24
  (111 shorter events, 21.2 us)
Async XLA Ops:
  8.0 0.7 copy-start.6
  8.0 136.5 %reduce-scatter.4.cloned.1.call-start = ((), (), s32[]{:S(2)}) async-start(), calls=%async_computation.2 | async-start | bytes 81920
  30.2 14.3 %copy-start.2 = (bf16[2,4,1024]{2,1,0:T(4,128)(2,1)S(1)}, bf16[2,4,1024]{2,1,0:T(4,128)(2,1)}, u32[]{:S(2)}) copy-start(bf16[2,4,1024]{2,1,0:T(4,128)(2,1)} %param.12) | copy-start | bytes 49156
  44.5 8.3 %copy-start.3 = (bf16[2,4,1024]{2,1,0:T(4,128)(2,1)S(1)}, bf16[2,4,1024]{2,1,0:T(4,128)(2,1)}, u32[]{:S(2)}) copy-start(bf16[2,4,1024]{2,1,0:T(4,128)(2,1)} %param.11) | copy-start | bytes 49156
  75.2 0.7 copy-start.4
  121.9 0.6 copy-start
  121.9 0.9 copy-start.1
  122.6 127.7 %all-reduce.3.cloned.1.call-start = ((), (), s32[]{:S(2)}) async-start(), calls=%async_computation.1 | async-start | bytes 262144 | tf_op jit(solution)/shard_map/psum | solution.py:39
  123.7 126.6 %copy-start.5 = (f32[1024]{0:T(1024)S(1)}, f32[1024]{0:T(1024)}, u32[]{:S(2)}) copy-start(f32[1024]{0:T(1024)} %param.13) | copy-start | bytes 12292
  123.7 126.7 %copy-start.7 = (f32[2,16]{1,0:T(2,128)S(1)}, f32[2,16]{1,0:T(2,128)}, u32[]{:S(2)}) copy-start(f32[2,16]{1,0:T(2,128)} %param.15) | copy-start | bytes 388
Sparse Core Ops, SparseCore 0:
  122.7 21.7 reduce-scatter.3
Sparse Core Ops, SparseCore 1:
  128.6 121.7 all-reduce.2
where the time goes:
time: 301 us; the launch traced here: 300 us
  waiting for transfers between devices  127 us (42%)
  blocking collectives  117 us (39%)
  local copies, waits for them, and re-layouts  21.7 us (7%)
  matrix products  16.1 us (5%)
  between operations  15.6 us (5%)
    psum x1, waiting for transfers between devices, on_device(): density = lax.psum(partial_density, ('row', 'col'))  106 us
    psum x1, blocking collectives, on_device(): alpha = lax.psum(gram, ('row', 'col')) / (total_count * band_count)  39.3 us
    unnamed x3, waiting for transfers between devices  20.8 us
    all_gather x1, blocking collectives, on_device(): lax.all_gather(valence, 'row', axis=0, tiled=True)  14.3 us
    all_gather x1, blocking collectives, on_device(): lax.all_gather(conduction, 'row', axis=0, tiled=True)  14 us
    all_gather x1, blocking collectives, on_device(): lax.all_gather(k_coords, 'row', axis=0, tiled=True)  13.5 us
    all_gather x1, blocking collectives, on_device(): lax.all_gather(vectors, 'row', axis=0, tiled=True)  12.8 us
    dot_general x8, matrix products, square_sweep(): jnp.einsum('ijg,jng->ing', coupling, col_proj, precision=highest)  8.7 us
  transfers between devices with their start and end apart: 2, of which 2 were waited for; matrix products, arithmetic and copies ran while one was open for 0% of the time, Pallas kernels for 0%

commit v1 on v0

--- a/solution.py
+++ b/solution.py
@@ -92,7 +92,7 @@
         - owned / total_count
     )
     gram = jnp.einsum("ktm,ktn->mn", moving_wide, applied, precision=highest)
-    alpha = lax.psum(gram, ("row", "col")) / (total_count * band_count)
+    alpha = jnp.sum(lax.all_gather(gram, ("row", "col")), axis=0) / (total_count * band_count)
     residual = applied - jnp.einsum("ktm,mn->ktn", moving_wide, alpha, precision=highest)
     return (residual.reshape(local_count, band_count * vector_count), alpha)
 

time: 301 us -> 330 us (1.096)
  blocking collectives: 117 us -> 146 us
    all_gather x0 -> x1, blocking collectives: none -> 68 us  [on_device(): lax.all_gather(gram, ('row', 'col'))]
    psum x1 -> x0, blocking collectives: 39.3 us -> none  [on_device(): alpha = lax.psum(gram, ('row', 'col')) / (total_count * band_count)]
where the time goes in v1:
time: 330 us; the launch traced here: 329 us
  blocking collectives  146 us (44%)
  waiting for transfers between devices  127 us (38%)
  local copies, waits for them, and re-layouts  21.9 us (7%)
  matrix products  16.1 us (5%)
  between operations  15.6 us (5%)
    psum x1, waiting for transfers between devices, on_device(): density = lax.psum(partial_density, ('row', 'col'))  106 us
    all_gather x1, blocking collectives, on_device(): lax.all_gather(gram, ('row', 'col'))  68 us
    unnamed x3, waiting for transfers between devices  20.8 us
    all_gather x1, blocking collectives, on_device(): lax.all_gather(valence, 'row', axis=0, tiled=True)  14.3 us
    all_gather x1, blocking collectives, on_device(): lax.all_gather(conduction, 'row', axis=0, tiled=True)  14 us
    all_gather x1, blocking collectives, on_device(): lax.all_gather(k_coords, 'row', axis=0, tiled=True)  13.5 us
    all_gather x1, blocking collectives, on_device(): lax.all_gather(vectors, 'row', axis=0, tiled=True)  12.8 us
    dot_general x8, matrix products, square_sweep(): jnp.einsum('ijg,jng->ing', coupling, col_proj, precision=highest)  8.7 us
  transfers between devices with their start and end apart: 2, of which 2 were waited for; matrix products, arithmetic and copies ran while one was open for 0% of the time, Pallas kernels for 0%

profile of v1, /device:TPU:0, one launch (start us, length us, event | category | flops | bytes accessed | tf_op | source)
XLA Modules:
  0.0 328.8 jit_solution(13574463554490786483)
XLA Ops:
  8.7 13.5 %all-gather.3 = s32[8,2,2]{2,1,0:T(2,128)S(1)} all-gather(s32[1,2,2]{2,1,0:T(2,128)S(1)} %bitcast.67), channel_id=1, replica_groups=mesh['row'=8,'col'=4] {'row'}, dimensions={0}, use_global_device_ids=true | all-gather | bytes 144 | tf_op jit(solution)/shard_map/all_gather | solution.py:46
  22.1 8.1 %all-gather.2 = s32[4,2,2]{2,1,0:T(2,128)S(1)} all-gather(s32[1,2,2]{2,1,0:T(2,128)S(1)} %bitcast.68), channel_id=1, replica_groups=mesh['row'=8,'col'=4] {'col'}, dimensions={0}, use_global_device_ids=true | all-gather | bytes 80 | tf_op jit(solution)/shard_map/all_gather | solution.py:51
  30.2 14.3 %all_gather.29 = bf16[16,4,1024]{2,1,0:T(4,128)(2,1)S(1)} all-gather(bf16[2,4,1024]{2,1,0:T(4,128)(2,1)} %param.12), channel_id=1, replica_groups=mesh['row'=8,'col'=4] {'row'}, dimensions={0}, use_global_device_ids=true | all-gather | bytes 147456 | tf_op jit(solution)/shard_map/all_gather | solution.py:44
  44.5 8.3 %all_gather.27 = bf16[8,4,1024]{2,1,0:T(4,128)(2,1)S(1)} all-gather(bf16[2,4,1024]{2,1,0:T(4,128)(2,1)S(1)} %copy-done.2), channel_id=1, replica_groups=mesh['row'=8,'col'=4] {'col'}, dimensions={0}, use_global_device_ids=true | all-gather | bytes 81920 | tf_op jit(solution)/shard_map/all_gather | solution.py:50
  52.9 14.0 %all_gather.30 = bf16[16,4,1024]{2,1,0:T(4,128)(2,1)S(1)} all-gather(bf16[2,4,1024]{2,1,0:T(4,128)(2,1)S(1)} %copy-done.3), channel_id=1, replica_groups=mesh['row'=8,'col'=4] {'row'}, dimensions={0}, use_global_device_ids=true | all-gather | bytes 147456 | tf_op jit(solution)/shard_map/all_gather | solution.py:43
  66.9 7.2 %all_gather.28 = bf16[8,4,1024]{2,1,0:T(4,128)(2,1)S(1)} all-gather(bf16[2,4,1024]{2,1,0:T(4,128)(2,1)S(1)} %copy-done.3), channel_id=1, replica_groups=mesh['row'=8,'col'=4] {'col'}, dimensions={0}, use_global_device_ids=true | all-gather | bytes 81920 | tf_op jit(solution)/shard_map/all_gather | solution.py:49
  75.8 12.8 %all-gather.1 = bf16[8,2,512]{2,1,0:T(2,128)(2,1)S(1)} all-gather(bf16[1,2,512]{2,1,0:T(2,128)(2,1)S(1)} %bitcast.66), channel_id=1, replica_groups=mesh['row'=8,'col'=4] {'row'}, dimensions={0}, use_global_device_ids=true | all-gather | bytes 18432 | tf_op jit(solution)/shard_map/all_gather | solution.py:45
  88.7 33.2 %while.14 = (s32[]{:T(128)}, f32[8,16,32]{2,1,0:T(8,128)S(1)}, bf16[8,16,1024]{2,1,0:T(8,128)(2,1)S(1)}, bf16[16,16,1024]{2,1,0:T(8,128)(2,1)S(1)}, bf16[16,16,3...) while((s32[]{:T(128)}, f32[8,16,32]{2,1,0:T(8,128)S(1)}, ...), condition=%wide.region_2.3_spmd.clone, body=%wide.region_1.2_spmd.clone.sunk | while | flops 14714503 | bytes 2319689 | solution.py:73
  88.7 0.7 constant_dynamic-slice_fusion.2
  89.6 0.6 gather_fusion
  91.4 1.1 convolution_bitcast_fusion.8
  92.9 0.7 constant_dynamic-slice_fusion.2
  95.5 1.1 convolution_bitcast_fusion.8
  97.0 0.7 constant_dynamic-slice_fusion.2
  99.7 1.1 convolution_bitcast_fusion.8
  101.2 0.7 constant_dynamic-slice_fusion.2
  103.8 1.1 convolution_bitcast_fusion.8
  105.3 0.7 constant_dynamic-slice_fusion.2
  108.0 1.1 convolution_bitcast_fusion.8
  109.5 0.7 constant_dynamic-slice_fusion.2
  112.1 1.1 convolution_bitcast_fusion.8
  113.6 0.7 constant_dynamic-slice_fusion.2
  116.3 1.1 convolution_bitcast_fusion.8
  117.8 0.7 constant_dynamic-slice_fusion.2
  120.4 1.1 convolution_bitcast_fusion.8
  122.8 0.9 convolution_bitcast_fusion.2
  123.7 20.8 %reduce-scatter.4.cloned.1.call-done = f32[1,2,16,32]{3,2,1,0:T(8,128)} async-done(((f32[4,2,16,32]{3,2,1,0:T(8,128)}), f32[1,2,16,32]{3,2,1,0:T(8,128)}) %reduce-scatter.4.cloned.1.call-update) | async-done | bytes 4112
  144.5 105.8 %all-reduce.3.cloned.1.call-done = f32[1024,32]{0,1:T(8,128)} async-done(((f32[1024,32]{0,1:T(8,128)}), f32[1024,32]{0,1:T(8,128)}) %all-reduce.3.cloned.1.call-update) | async-done | bytes 131088 | tf_op jit(solution)/shard_map/psum | solution.py:39
  250.3 1.1 fusion.17
  251.7 68.0 %all-gather = f32[1024,32]{1,0:T(8,128)S(1)} all-gather(f32[32,32]{1,0:T(8,128)S(1)} %copy.19), channel_id=2, replica_groups=mesh['row'=8,'col'=4] {'row','col'}, dimensions={0}, use_global_device_ids=true | all-gather | bytes 135168 | tf_op jit(solution)/shard_map/all_gather | solution.py:95
  320.0 0.7 reshape.61
  320.7 0.7 copy.22
  (114 shorter events, 21.4 us)
Async XLA Ops:
  8.0 0.7 copy-start.6
  8.0 136.5 %reduce-scatter.4.cloned.1.call-start = ((), (), s32[]{:S(2)}) async-start(), calls=%async_computation.2 | async-start | bytes 81920
  30.2 14.3 %copy-start.2 = (bf16[2,4,1024]{2,1,0:T(4,128)(2,1)S(1)}, bf16[2,4,1024]{2,1,0:T(4,128)(2,1)}, u32[]{:S(2)}) copy-start(bf16[2,4,1024]{2,1,0:T(4,128)(2,1)} %param.12) | copy-start | bytes 49156
  44.5 8.3 %copy-start.3 = (bf16[2,4,1024]{2,1,0:T(4,128)(2,1)S(1)}, bf16[2,4,1024]{2,1,0:T(4,128)(2,1)}, u32[]{:S(2)}) copy-start(bf16[2,4,1024]{2,1,0:T(4,128)(2,1)} %param.11) | copy-start | bytes 49156
  75.2 0.7 copy-start.4
  121.9 0.6 copy-start
  121.9 0.9 copy-start.1
  122.6 127.7 %all-reduce.3.cloned.1.call-start = ((), (), s32[]{:S(2)}) async-start(), calls=%async_computation.1 | async-start | bytes 262144 | tf_op jit(solution)/shard_map/psum | solution.py:39
  123.7 126.6 %copy-start.5 = (f32[1024]{0:T(1024)S(1)}, f32[1024]{0:T(1024)}, u32[]{:S(2)}) copy-start(f32[1024]{0:T(1024)} %param.13) | copy-start | bytes 12292
  123.7 126.6 %copy-start.7 = (f32[2,16]{1,0:T(2,128)S(1)}, f32[2,16]{1,0:T(2,128)}, u32[]{:S(2)}) copy-start(f32[2,16]{1,0:T(2,128)} %param.15) | copy-start | bytes 388
Sparse Core Ops, SparseCore 0:
  122.7 21.7 reduce-scatter.3
Sparse Core Ops, SparseCore 1:
  128.6 121.6 all-reduce.2
